TPU v7x, 256 devices: a whole 4x4x8 slice. The times are simulated.
256 devices in a mesh: grp: 16 (over z_lo, y, core), seq: 16 (over z_hi, x).
Axes of the slice: x: 4, y: 4, z: 8 (z_hi: 4, z_lo: 2; z = z_hi * 2 + z_lo), core: 2. Of those that a mesh axis runs over, the one named last changes fastest.
Arguments:
- query: bfloat16 [16, 4096, 640], P('grp', 'seq'), may hold values from -64 to 64
- resp_kv: bfloat16 [16, 4096, 256], P('grp', 'seq'), may hold values from -6 to 6
- prompt_kv: bfloat16 [16, 4096, 256], P('grp', 'seq'), may hold values from -64 to 64
- grad_out: bfloat16 [16, 4096, 640], P('grp', 'seq'), may hold values from -6 to 6
- rewards: float32 [16, 16], P('grp'), may hold values from -4 to 4
- lengths: int32 [16, 16], P('grp'), may hold values from 1 to 256, as said below
- block_order: int32 [16, 32], P('grp'), may hold values from 0 to 31, each once within a row
Outputs:
- grad_query: bfloat16 [16, 4096, 640], P('grp', 'seq')
- grad_stream: bfloat16 [16, 4096, 256], P('grp', 'seq')
- grad_prompt: bfloat16 [16, 4096, 256], P('grp', 'seq')
Inputs may be any that keep to these rules, and one draw needn't show every extreme that they name: `lengths`: each response has 1 to 256 tokens; some response has exactly 256. Each row of block_order names every response block of its group once.
All inputs are finite; a program needn't handle non-finite values.
Results may differ from a plain program's by a relative error of at most 0.015.
Values may be sent and summed in bfloat16 or wider, within the bound.
A program may use at most 128 MiB of HBM per device.

v0:
```python
import jax
import jax.numpy as jnp
from jax import lax
from jax.experimental import pallas as pl
from jax.experimental.pallas import tpu as pltpu
from jax.sharding import PartitionSpec as P

RESP = 16
BLK = 128
NB = 2
HD = 128
QPK = 5
LOSS_SCALE = 32.0
NEG = -1e30
LOG2E = 1.4426950408889634
MESH = pl.DeviceIdType.MESH
F32 = jnp.float32
BF16 = jnp.bfloat16

SIDE = 4
MEMBERS = SIDE * SIDE
CHUNK = NB * BLK
ROWS = NB * QPK * BLK
TILES = NB * QPK
WIDE = 256

UP = pl.ds(0, BLK)
DOWN = pl.ds(BLK, BLK)
KEYS = pl.ds(0, HD)
VALUES = pl.ds(HD, HD)
OWN = MEMBERS

GATHER_ORDER = (
    (0, 0), (0, 1), (0, 3), (0, 2), (3, 0), (1, 0), (1, 1), (1, 3),
    (3, 1), (3, 3), (2, 0), (2, 1), (2, 3), (3, 2), (1, 2), (2, 2),
)
REDUCE_ORDER = (
    (2, 2), (3, 2), (1, 2), (2, 1), (2, 3), (2, 0), (1, 1), (3, 1),
    (1, 3), (3, 3), (1, 0), (3, 0), (0, 2), (0, 1), (0, 3), (0, 0),
)
N_COPIES = 58


def dot(a, b):
    return jnp.dot(a, b, preferred_element_type=F32)


def wrapped(t, n):
    return t - jnp.where(t >= n, n, 0)


def slot_at(sequence, step):
    slot = jnp.int32(0)
    for k, (a, b) in enumerate(sequence):
        slot = slot + jnp.where(step == k, a * SIDE + b, 0)
    return slot


def kernel(
    query_hbm, resp_hbm, prompt_hbm, grad_out_hbm, rewards_hbm, lengths_hbm, order_hbm,
    grad_query, grad_stream, grad_prompt,
    query, grad_out, resp, rewards, lengths, order, partner,
    kv, scores, dprobs, q_rows, w_rows, q_cols, w_cols,
    peak, total, weigh, p_low, ds_low, dq_cols, g_tmp, g_send, g_hold,
    x_rel_a, x_rel_b, x_in_l, x_in_r, x_sum,
    z_send, z_rel_a, z_rel_b, z_in_l, z_in_r, z_far,
    table_a, send_b, partner_kv, table_c, send_d, partner_grad, give, own_grad,
    count_send, count_recv,
    ssem, rsem, esend, erecv, csend, crecv, isem, known,
):
    scale = HD ** (-0.5)
    c = scale * LOG2E
    me = lax.axis_index("seq")
    grp = lax.axis_index("grp")
    z, x = me // SIDE, me % SIDE
    right = z * SIDE + (x + 1) % SIDE
    left = z * SIDE + (x + SIDE - 1) % SIDE
    above = ((z + 1) % SIDE) * SIDE + x
    below = ((z + SIDE - 1) % SIDE) * SIDE + x

    inputs = [
        pltpu.make_async_copy(src, dst, isem.at[k])
        for k, (src, dst) in enumerate((
            (prompt_hbm, kv.at[0]), (resp_hbm, resp), (order_hbm, order), (lengths_hbm, lengths),
            (rewards_hbm, rewards), (query_hbm, query), (grad_out_hbm, grad_out),
        ))
    ]
    for load in inputs:
        load.start()

    copies = {}

    def declare(name, src, dst, dev):
        k = len(copies)
        copies[name] = pltpu.make_async_remote_copy(
            src_ref=src, dst_ref=dst, send_sem=ssem.at[k], recv_sem=rsem.at[k],
            device_id={"seq": dev}, device_id_type=MESH,
        )

    def slot_ref(a, b, half):
        return kv.at[a * SIDE + b, half]

    halves = (UP, DOWN)
    for a in range(SIDE):
        for h in range(2):
            declare(("R", a, h), slot_ref(a, 0, halves[h]), slot_ref(a, 3, halves[h]), right)
            declare(("L", a, h), slot_ref(a, 0, halves[h]), slot_ref(a, 1, halves[h]), left)
            declare(("gr", a, h), g_send.at[a * SIDE + 1, halves[h]], x_in_l.at[a, halves[h]], right)
            declare(("gl", a, h), g_send.at[a * SIDE + 3, halves[h]], x_in_r.at[a, halves[h]], left)
        if a != 1:
            declare(("FR", a), slot_ref(a, 3, UP), slot_ref(a, 2, UP), right)
        if a != 3:
            declare(("FL", a), slot_ref(a, 1, DOWN), slot_ref(a, 2, DOWN), left)
        if a % 2 == 0:
            declare(("r", a), g_send.at[a * SIDE + 2, UP], x_rel_a.at[a // 2], right)
            declare(("l", a), g_send.at[a * SIDE + 2, DOWN], x_rel_b.at[a // 2], left)
    for h in range(2):
        declare(("U", h), slot_ref(0, 0, halves[h]), slot_ref(3, 0, halves[h]), above)
        declare(("D", h), slot_ref(0, 0, halves[h]), slot_ref(1, 0, halves[h]), below)
        declare(("zu", h), z_send.at[1, halves[h]], z_in_l.at[halves[h]], above)
        declare(("zd", h), z_send.at[3, halves[h]], z_in_r.at[halves[h]], below)
    declare(("VU",), slot_ref(0, 2, DOWN), slot_ref(3, 2, DOWN), above)
    declare(("VD",), slot_ref(0, 2, UP), slot_ref(1, 2, UP), below)
    declare(("yu",), g_send.at[SIDE + 2], z_far.at[0], above)
    declare(("yd",), g_send.at[3 * SIDE + 2], z_far.at[1], below)
    declare(("FU",), slot_ref(3, 0, UP), slot_ref(2, 0, UP), above)
    declare(("FD",), slot_ref(1, 0, DOWN), slot_ref(2, 0, DOWN), below)
    declare(("zr",), z_send.at[2, UP], z_rel_a, above)
    declare(("zl",), z_send.at[2, DOWN], z_rel_b, below)

    def start(*names):
        for name in names:
            copies[name].start()

    def arrived(*names):
        for name in names:
            copies[name].wait_recv()

    def piece(t):
        second = jnp.where(t >= MEMBERS // 2, 1, 0)
        return (
            slice(None),
            pl.ds(pl.multiple_of((t - second * (MEMBERS // 2)) * 16, 16), 16),
            pl.ds(pl.multiple_of(second * HD, HD), HD),
        )

    def spread_copy(stage, src, dst, k):
        t = wrapped(me + k, MEMBERS)
        return pltpu.make_async_remote_copy(
            src_ref=src.at[piece(t)], dst_ref=dst.at[pl.ds(NB * k, NB)],
            send_sem=esend.at[stage, k], recv_sem=erecv.at[stage, k],
            device_id={"seq": t}, device_id_type=MESH,
        )

    def deliver_copy(stage, src, dst, k):
        t = wrapped(me + k, MEMBERS)
        return pltpu.make_async_remote_copy(
            src_ref=src.at[pl.ds(NB * k, NB)], dst_ref=dst.at[piece(me)],
            send_sem=esend.at[stage, k], recv_sem=erecv.at[stage, k],
            device_id={"seq": t}, device_id_type=MESH,
        )

    def every(fn):
        def body(k, carry):
            fn(k)
            return carry

        lax.fori_loop(1, MEMBERS, body, 0)

    def spread(stage, src, dst):
        every(lambda k: spread_copy(stage, src, dst, k).start())
        dst[pl.ds(0, NB)] = src[piece(me)]

    def deliver(stage, table, buf, dst):
        def fill(k, carry):
            for i in range(NB):
                buf[NB * k + i] = table[partner[NB * wrapped(me + k, MEMBERS) + i]]
            return carry

        lax.fori_loop(0, MEMBERS, fill, 0)
        every(lambda k: deliver_copy(stage, buf, dst, k).start())
        dst[piece(me)] = buf[pl.ds(0, NB)]

    def find_partners():
        def one(j, carry):
            b = order[j]
            sibling = b + 1 - 2 * lax.rem(b, NB)
            found = jnp.int32(0)
            for k in range(MEMBERS):
                far = wrapped(me + MEMBERS - k, MEMBERS) * NB
                for i in range(NB):
                    found = found + jnp.where(order[NB * k + i] == sibling, far + i, 0)
            partner[j] = found
            return carry

        lax.fori_loop(0, NB * MEMBERS, one, 0)

    mate = grp + 1 - 2 * (grp % 2)
    y_next = (grp // 8) * 8 + (grp % 8 + 2) % 8
    y_last = (grp // 8) * 8 + (grp % 8 + 6) % 8
    z_mate = (grp + 8) % 16
    counts = [
        pltpu.make_async_remote_copy(
            src_ref=src, dst_ref=count_recv.at[k], send_sem=csend.at[k], recv_sem=crecv.at[k],
            device_id={"grp": peer}, device_id_type=MESH,
        )
        for k, (src, peer) in enumerate((
            (count_send.at[0], mate), (count_send.at[1], y_next), (count_send.at[1], y_last),
            (count_recv.at[1], y_next), (count_send.at[2], z_mate),
        ))
    ]

    neighbours = (right, left, above, below)
    barrier = pltpu.get_barrier_semaphore()
    for dev in neighbours:
        pl.semaphore_signal(barrier, inc=1, device_id={"seq": dev}, device_id_type=MESH)
    for dev in (mate, y_next, y_last, z_mate):
        pl.semaphore_signal(barrier, inc=1, device_id={"grp": dev}, device_id_type=MESH)

    def pass_on(k):
        for dev in neighbours:
            pl.semaphore_signal(known.at[k], inc=1, device_id={"seq": dev}, device_id_type=MESH)

    def heard(k):
        pl.semaphore_wait(known.at[k], len(neighbours))

    inputs[0].wait()
    pl.semaphore_wait(barrier, 8)

    start(("U", 0), ("D", 1), ("R", 0, 0), ("L", 0, 1), ("U", 1), ("D", 0), ("R", 0, 1), ("L", 0, 0))
    pass_on(0)
    for load in inputs[1:]:
        load.wait()
    tokens = lengths[0]
    for r in range(1, RESP):
        tokens = tokens + lengths[r]
    count_send[0] = jnp.full((8, HD), tokens, jnp.int32)
    counts[0].start()
    heard(0)
    pass_on(1)

    mean = rewards[0]
    for r in range(1, RESP):
        mean = mean + rewards[r]
    mean = mean * (1.0 / RESP)
    is_later = []
    row_number = lax.broadcasted_iota(jnp.int32, (BLK, HD), 0)
    for i in range(NB):
        b = order[NB * me + i]
        r, h = b // NB, b % NB
        is_later.append(h)
        gain = jnp.where(row_number + h * BLK < lengths[r], rewards[r] - mean, 0.0)
        for head in range(QPK):
            tile = pl.ds((i * QPK + head) * BLK, BLK)
            rows = pl.ds(i * BLK, BLK)
            cols = pl.ds(head * HD, HD)
            q = query[rows, cols].astype(F32)
            w = grad_out[rows, cols].astype(F32) * gain
            q_rows[tile, :] = q.astype(BF16)
            w_rows[tile, :] = w.astype(BF16)
            q_cols[:, tile] = q.T.astype(BF16)
            w_cols[:, tile] = w.T.astype(BF16)
    heard(1)
    pass_on(2)
    find_partners()
    peak[...] = jnp.full_like(peak, NEG)
    total[...] = jnp.zeros_like(total)
    weigh[...] = jnp.zeros_like(weigh)
    dq_cols[...] = jnp.zeros_like(dq_cols)

    def take_in(slot):
        for n in range(TILES):
            tile = pl.ds(n * BLK, BLK)
            s = scores[slot, :, tile].reshape(CHUNK // 8, 8, BLK)
            d = dprobs[slot, :, tile].reshape(CHUNK // 8, 8, BLK)
            before = peak[:, tile]
            now = jnp.maximum(before, jnp.max(s, axis=0))
            fade = jnp.exp2((before - now) * c)
            e = jnp.exp2((s - now[None]) * c)
            total[:, tile] = total[:, tile] * fade + jnp.sum(e, axis=0)
            weigh[:, tile] = weigh[:, tile] * fade + jnp.sum(e * d, axis=0)
            peak[:, tile] = now

    def own_pair(i, cols):
        return jnp.concatenate([resp[i, :, cols], partner_kv[i, :, cols]], axis=0)

    def own_scores():
        key = lax.broadcasted_iota(jnp.int32, (CHUNK, BLK), 0)
        pos = lax.broadcasted_iota(jnp.int32, (CHUNK, BLK), 1)
        for i in range(NB):
            limit = jnp.where(is_later[i] == 1, CHUNK, BLK)
            seen = jnp.where(key < BLK, pos - key, limit - 1 - key) >= 0
            k_own, v_own = own_pair(i, KEYS), own_pair(i, VALUES)
            for head in range(QPK):
                tile = pl.ds((i * QPK + head) * BLK, BLK)
                scores[OWN, :, tile] = jnp.where(seen, dot(k_own, q_cols[:, tile]), NEG)
                dprobs[OWN, :, tile] = dot(v_own, w_cols[:, tile])
        take_in(OWN)

    def gather_events(s):
        if s == 1:
            arrived(("R", 0, 0), ("L", 0, 1))
            start(("FR", 0), ("FL", 0))
            heard(2)
            spread(0, resp, table_a)
            arrived(("U", 0), ("D", 1))
            start(("FU",), ("FD",), ("R", 3, 0), ("L", 1, 1), ("R", 1, 1), ("L", 3, 0))
            arrived(("R", 0, 1), ("L", 0, 0))
        elif s == 3:
            arrived(("FR", 0), ("FL", 0))
            start(("VU",), ("VD",))
            counts[0].wait_recv()
            count_send[1] = count_send[0] + count_recv[0]
            counts[1].start()
            counts[2].start()
        elif s == 4:
            arrived(("U", 1), ("D", 0))
            start(("R", 1, 0), ("L", 3, 1), ("R", 3, 1), ("L", 1, 0))
        elif s == 6:
            arrived(("R", 3, 0), ("L", 1, 1))
            start(("FR", 3), ("FL", 1))
            arrived(("L", 1, 0))
        elif s == 7:
            arrived(("FU",), ("FD",))
            start(("R", 2, 0), ("L", 2, 1), ("R", 2, 1), ("L", 2, 0))
            every(lambda k: spread_copy(0, resp, table_a, k).wait_recv())
            deliver(1, table_a, send_b, partner_kv)
            arrived(("R", 1, 0), ("R", 1, 1))
        elif s == 8:
            arrived(("L", 3, 1), ("L", 3, 0))
            counts[1].wait_recv()
            counts[2].wait_recv()
            counts[3].start()
        elif s == 9:
            arrived(("R", 3, 1))
        elif s == 11:
            arrived(("R", 2, 0), ("L", 2, 1))
            start(("FR", 2), ("FL", 2))
            arrived(("L", 2, 0))
        elif s == 12:
            arrived(("R", 2, 1))
            counts[3].wait_recv()
            count_send[2] = count_send[1] + count_recv[1] + count_recv[2] + count_recv[3]
            counts[4].start()
        elif s == 13:
            arrived(("VU",), ("FR", 3))
        elif s == 14:
            arrived(("VD",), ("FL", 1))
        elif s == 15:
            every(lambda k: deliver_copy(1, send_b, partner_kv, k).wait_recv())
            own_scores()
            arrived(("FR", 2), ("FL", 2))

    def gather_step(s, carry):
        for k in (1, 3, 4, 6, 7, 8, 9, 11, 12, 13, 14, 15):
            @pl.when(s == k)
            def _(k=k):
                gather_events(k)

        slot = slot_at(GATHER_ORDER, s)
        keys, values = kv[slot, :, KEYS], kv[slot, :, VALUES]
        for n in range(ROWS // WIDE):
            tile = pl.ds(n * WIDE, WIDE)
            scores[slot, :, tile] = dot(keys, q_cols[:, tile])
            dprobs[slot, :, tile] = dot(values, w_cols[:, tile])
        take_in(slot)
        return carry

    lax.fori_loop(0, MEMBERS, gather_step, 0)

    for n in range(TILES):
        tile = pl.ds(n * BLK, BLK)
        m = peak[:, tile]
        top = jnp.max(m, axis=0, keepdims=True)
        fade = jnp.exp2((m - top) * c)
        mass = jnp.sum(total[:, tile] * fade, axis=0, keepdims=True)
        delta = jnp.sum(weigh[:, tile] * fade, axis=0, keepdims=True) / mass
        peak[:, tile] = jnp.broadcast_to(top + jnp.log2(mass) * (1.0 / c), (8, BLK))
        weigh[:, tile] = jnp.broadcast_to(delta, (8, BLK))

    def probabilities(slot):
        for n in range(TILES):
            tile = pl.ds(n * BLK, BLK)
            s = scores[slot, :, tile].reshape(CHUNK // 8, 8, BLK)
            d = dprobs[slot, :, tile].reshape(CHUNK // 8, 8, BLK)
            p = jnp.exp2((s - peak[:, tile][None]) * c)
            ds = p * (d - weigh[:, tile][None])
            p_low[:, tile] = p.reshape(CHUNK, BLK).astype(BF16)
            ds_low[:, tile] = ds.reshape(CHUNK, BLK).astype(BF16)

    def add_query_grad(keys, tile):
        dq_cols[:, tile] += lax.dot_general(
            keys, ds_low[:, tile], (((0,), (0,)), ((), ())), preferred_element_type=F32
        )

    def own_grads():
        probabilities(OWN)
        for i in range(NB):
            tile = pl.ds(i * QPK * BLK, QPK * BLK)
            d_keys = dot(ds_low[:, tile], q_rows[tile, :])
            d_values = dot(p_low[:, tile], w_rows[tile, :])
            add_query_grad(own_pair(i, KEYS), tile)
            own_grad[i, :, KEYS] = d_keys[:BLK]
            own_grad[i, :, VALUES] = d_values[:BLK]
            give[i, :, KEYS] = d_keys[BLK:].astype(BF16)
            give[i, :, VALUES] = d_values[BLK:].astype(BF16)
        spread(2, give, table_c)

    def keep(a, b, h):
        g_send[a * SIDE + b, halves[h]] = g_tmp[halves[h]].astype(BF16)

    def join_right(a):
        arrived(("r", a))
        g_send[a * SIDE + 1, UP] = (g_hold[a] + x_rel_a[a // 2].astype(F32)).astype(BF16)
        start(("gr", a, 0))

    def join_left(a):
        arrived(("l", a))
        g_send[a * SIDE + 3, DOWN] = (g_hold[a + 1] + x_rel_b[a // 2].astype(F32)).astype(BF16)
        start(("gl", a, 1))

    def x_combined(a, h):
        arrived(("gr", a, h), ("gl", a, h))
        half = halves[h]
        return x_sum[a, half] + x_in_l[a, half].astype(F32) + x_in_r[a, half].astype(F32)

    def reduce_events(p):
        a, b = REDUCE_ORDER[p]
        if b == 0:
            x_sum[a] = g_tmp[...]
        elif (a, b) == (0, 2):
            arrived(("yu",), ("yd",))
            g_send[2] = (g_tmp[...] + z_far[0].astype(F32) + z_far[1].astype(F32)).astype(BF16)
        elif a % 2 or b == 2:
            keep(a, b, 0)
            keep(a, b, 1)
        elif b == 1:
            keep(a, 1, 1)
            g_hold[a] = g_tmp[UP]
        else:
            keep(a, 3, 0)
            g_hold[a + 1] = g_tmp[DOWN]
        if p == 0:
            start(("r", 2), ("l", 2))
        elif p == 1:
            start(("yd",))
        elif p == 2:
            start(("yu",))
        elif p == 3:
            start(("gr", 2, 1))
        elif p == 4:
            start(("gl", 2, 0))
            join_right(2)
            join_left(2)
        elif p == 5:
            own_grads()
        elif p == 6:
            start(("gr", 1, 1))
        elif p == 7:
            start(("gr", 3, 0), ("gr", 1, 0), ("gr", 3, 1))
        elif p == 8:
            start(("gl", 1, 1))
        elif p == 9:
            start(("gl", 3, 0), ("gl", 1, 0), ("gl", 3, 1))
            for h in range(2):
                z_send[2, halves[h]] = x_combined(2, h).astype(BF16)
            start(("zr",), ("zl",))
        elif p == 12:
            start(("r", 0), ("l", 0))
            z_send[1, DOWN] = x_combined(1, 1).astype(BF16)
            start(("zu", 1))
            z_send[3, UP] = x_combined(3, 0).astype(BF16)
            start(("zd", 0))
        elif p == 13:
            start(("gr", 0, 1))
            every(lambda k: spread_copy(2, give, table_c, k).wait_recv())
            deliver(3, table_c, send_d, partner_grad)
        elif p == 14:
            start(("gl", 0, 0))
            join_right(0)
            join_left(0)
            value = x_combined(1, 0)
            arrived(("zr",))
            z_send[1, UP] = (value + z_rel_a[...].astype(F32)).astype(BF16)
            start(("zu", 0))
            value = x_combined(3, 1)
            arrived(("zl",))
            z_send[3, DOWN] = (value + z_rel_b[...].astype(F32)).astype(BF16)
            start(("zd", 1))

    def reduce_step(p, carry):
        slot = slot_at(REDUCE_ORDER, p)
        probabilities(slot)
        g_tmp[:, KEYS] = dot(ds_low[...], q_rows[...])
        g_tmp[:, VALUES] = dot(p_low[...], w_rows[...])
        for n in range(ROWS // WIDE):
            add_query_grad(kv[slot, :, KEYS], pl.ds(n * WIDE, WIDE))

        for k in range(MEMBERS):
            @pl.when(p == k)
            def _(k=k):
                reduce_events(k)

        return carry

    lax.fori_loop(0, MEMBERS, reduce_step, 0)

    counts[4].wait_recv()
    tokens = (count_send[2] + count_recv[4]).astype(F32)
    factor = (LOSS_SCALE * 16 * RESP * CHUNK) / tokens[0:1]
    for i in range(NB):
        for head in range(QPK):
            rows = pl.ds(i * BLK, BLK)
            grads = dq_cols[:, pl.ds((i * QPK + head) * BLK, BLK)]
            grad_query[rows, pl.ds(head * HD, HD)] = (grads.T * (factor * scale)).astype(BF16)

    every(lambda k: deliver_copy(3, send_d, partner_grad, k).wait_recv())
    stream = own_grad[...] + partner_grad[...].astype(F32)
    grad_stream[:, :, KEYS] = (stream[:, :, :HD] * (factor * scale)[None]).astype(BF16)
    grad_stream[:, :, VALUES] = (stream[:, :, HD:] * factor[None]).astype(BF16)

    for h in range(2):
        own = x_combined(0, h)
        arrived(("zu", h), ("zd", h))
        own = own + z_in_l[halves[h]].astype(F32) + z_in_r[halves[h]].astype(F32)
        grad_prompt[halves[h], KEYS] = (own[:, :HD] * (factor * scale)).astype(BF16)
        grad_prompt[halves[h], VALUES] = (own[:, HD:] * factor).astype(BF16)

    for name in copies:
        copies[name].wait_send()
    every(lambda k: spread_copy(0, resp, table_a, k).wait_send())
    every(lambda k: deliver_copy(1, send_b, partner_kv, k).wait_send())
    every(lambda k: spread_copy(2, give, table_c, k).wait_send())
    every(lambda k: deliver_copy(3, send_d, partner_grad, k).wait_send())
    for cp in counts:
        cp.wait_send()


def local(query, resp_kv, prompt_kv, grad_out, rewards, lengths, block_order):
    vmem = pl.BlockSpec(memory_space=pltpu.VMEM)
    hbm = pl.BlockSpec(memory_space=pl.ANY)
    pair = (CHUNK, 2 * HD)
    half = (BLK, 2 * HD)
    blocks = (NB, BLK, 2 * HD)
    pieces = (NB * MEMBERS, 16, HD)
    wide = (CHUNK, QPK * HD)
    grads = pl.pallas_call(
        kernel,
        name="attention_step",
        out_shape=(
            pltpu.VMEM(wide, BF16),
            pltpu.VMEM(blocks, BF16),
            pltpu.VMEM(pair, BF16),
        ),
        in_specs=[hbm] * 7,
        out_specs=(vmem,) * 3,
        scratch_shapes=[
            pltpu.VMEM(wide, BF16),
            pltpu.VMEM(wide, BF16),
            pltpu.VMEM(blocks, BF16),
            pltpu.SMEM((RESP,), F32),
            pltpu.SMEM((RESP,), jnp.int32),
            pltpu.SMEM((NB * MEMBERS,), jnp.int32),
            pltpu.SMEM((NB * MEMBERS,), jnp.int32),
            pltpu.VMEM((MEMBERS, *pair), BF16),
            pltpu.VMEM((MEMBERS + 1, CHUNK, ROWS), F32),
            pltpu.VMEM((MEMBERS + 1, CHUNK, ROWS), F32),
            pltpu.VMEM((ROWS, HD), BF16),
            pltpu.VMEM((ROWS, HD), BF16),
            pltpu.VMEM((HD, ROWS), BF16),
            pltpu.VMEM((HD, ROWS), BF16),
            pltpu.VMEM((8, ROWS), F32),
            pltpu.VMEM((8, ROWS), F32),
            pltpu.VMEM((8, ROWS), F32),
            pltpu.VMEM((CHUNK, ROWS), BF16),
            pltpu.VMEM((CHUNK, ROWS), BF16),
            pltpu.VMEM((HD, ROWS), F32),
            pltpu.VMEM(pair, F32),
            pltpu.VMEM((MEMBERS, *pair), BF16),
            pltpu.VMEM((4, *half), F32),
            pltpu.VMEM((2, *half), BF16),
            pltpu.VMEM((2, *half), BF16),
            pltpu.VMEM((SIDE, *pair), BF16),
            pltpu.VMEM((SIDE, *pair), BF16),
            pltpu.VMEM((SIDE, *pair), F32),
            pltpu.VMEM((SIDE, *pair), BF16),
            pltpu.VMEM(half, BF16),
            pltpu.VMEM(half, BF16),
            pltpu.VMEM(pair, BF16),
            pltpu.VMEM(pair, BF16),
            pltpu.VMEM((2, *pair), BF16),
            pltpu.VMEM(pieces, BF16),
            pltpu.VMEM(pieces, BF16),
            pltpu.VMEM(blocks, BF16),
            pltpu.VMEM(pieces, BF16),
            pltpu.VMEM(pieces, BF16),
            pltpu.VMEM(blocks, BF16),
            pltpu.VMEM(blocks, BF16),
            pltpu.VMEM(blocks, F32),
            pltpu.VMEM((3, 8, HD), jnp.int32),
            pltpu.VMEM((5, 8, HD), jnp.int32),
            pltpu.SemaphoreType.DMA((N_COPIES,)),
            pltpu.SemaphoreType.DMA((N_COPIES,)),
            pltpu.SemaphoreType.DMA((4, MEMBERS)),
            pltpu.SemaphoreType.DMA((4, MEMBERS)),
            pltpu.SemaphoreType.DMA((5,)),
            pltpu.SemaphoreType.DMA((5,)),
            pltpu.SemaphoreType.DMA((7,)),
            pltpu.SemaphoreType.REGULAR((3,)),
        ],
        compiler_params=pltpu.CompilerParams(
            collective_id=0, has_side_effects=True, vmem_limit_bytes=58 * 2**20
        ),
    )(
        query[0], resp_kv[0].reshape(blocks), prompt_kv[0], grad_out[0],
        rewards[0], lengths[0], block_order[0],
    )
    return grads[0][None], grads[1].reshape(1, *pair), grads[2][None]


def solution(mesh):
    rows = P("grp", "seq", None)
    small = P("grp", None)
    return jax.shard_map(
        local,
        mesh=mesh,
        in_specs=(rows, rows, rows, rows, small, small, small),
        out_specs=(rows, rows, rows),
        check_vma=False,
    )
```

profile of v0, /device:TPU:2, one launch (start us, length us, event | category | flops | bytes accessed | tf_op | source)
XLA Modules:
  0.0 63.2 jit_solution(17227241610718002929)
XLA Ops:
  0.6 60.6 %attention_step.1 = (bf16[256,640]{1,0:T(8,128)(2,1)S(1)}, bf16[2,128,256]{2,1,0:T(8,128)(2,1)S(1)}, bf16[256,256]{1,0:T(8,128)(2,1)S(1)}) custom-call(bf16[256,640]{1,0:T(8,128)(2,1)} %bitcast.13, bf16[2,128,256]{2,1,0:T(8,128)(2,1)} %bitcast.15, bf16[256,256]{1,0:T(8,128)(2,1)} %bitcast.16, bf16[256,640]{1,0:T(8,128)(2,1)} %bitcast.14, f32[16]{0:T(128)} %bitcast.17, ...), custom_call_target="tpu_custom_call" | custom-call | tf_op jit(solution)/shard_map/attention_step/pallas_call | solution.py:547
  61.2 0.7 %copy.13 = bf16[1,256,640]{2,1,0:T(8,128)(2,1)} copy(bf16[1,256,640]{2,1,0:T(8,128)(2,1)S(1)} %bitcast.10) | data formatting | bytes 655360
  61.9 0.7 %copy.14 = bf16[1,256,256]{2,1,0:T(8,128)(2,1)} copy(bf16[1,256,256]{2,1,0:T(8,128)(2,1)S(1)} %bitcast.12) | data formatting | bytes 262144
  62.6 0.7 %copy.15 = bf16[1,256,256]{2,1,0:T(8,128)(2,1)} copy(bf16[1,256,256]{2,1,0:T(8,128)(2,1)S(1)} %bitcast.11) | data formatting | bytes 262144
where the time goes:
time: 63.3 us; the launch traced here: 63.2 us
  Pallas kernels  60.6 us (96%)
  local copies, waits for them, and re-layouts  2.04 us (3%)
  between operations  0.64 us (1%)
    pallas_call x1, Pallas kernels, local(): pl.pallas_call(kernel, name='attention_step', out_shape=(pltpu.VMEM(wide,...  60.6 us
    unnamed x3, local copies, waits for them, and re-layouts  2.04 us

commit v1 on v0

--- a/solution.py
+++ b/solution.py
@@ -38,7 +38,25 @@
     (2, 2), (3, 2), (1, 2), (2, 1), (2, 3), (2, 0), (1, 1), (3, 1),
     (1, 3), (3, 3), (1, 0), (3, 0), (0, 2), (0, 1), (0, 3), (0, 0),
 )
-N_COPIES = 58
+REDUCE_EVENTS = (
+    (("far", 2),),
+    (("far", 3),),
+    (("far", 1),),
+    (("gr", 2, 1),),
+    (("gl", 2, 0), ("gr", 2, 0), ("gl", 2, 1)),
+    (("own",), ("spread",)),
+    (("gr", 1, 1),),
+    (("gr", 3, 0), ("gr", 1, 0), ("gr", 3, 1)),
+    (("gl", 1, 1),),
+    (("gl", 3, 0), ("gl", 1, 0), ("gl", 3, 1), ("z", 2, 0), ("z", 2, 1)),
+    (),
+    (),
+    (("far", 0), ("z", 1, 1), ("z", 3, 0), ("deliver",)),
+    (("gr", 0, 1),),
+    (("gl", 0, 0), ("z", 1, 0), ("z", 3, 1), ("gr", 0, 0), ("gl", 0, 1)),
+    (),
+)
+N_COPIES = 60
 
 
 def dot(a, b):
@@ -63,7 +81,7 @@
     kv, scores, dprobs, q_rows, w_rows, q_cols, w_cols,
     peak, total, weigh, p_low, ds_low, dq_cols, g_tmp, g_send, g_hold,
     x_rel_a, x_rel_b, x_in_l, x_in_r, x_sum,
-    z_send, z_rel_a, z_rel_b, z_in_l, z_in_r, z_far,
+    z_send, z_rel, z_in_l, z_in_r, z_far,
     table_a, send_b, partner_kv, table_c, send_d, partner_grad, give, own_grad,
     count_send, count_recv,
     ssem, rsem, esend, erecv, csend, crecv, isem, known,
@@ -111,9 +129,10 @@
             declare(("FR", a), slot_ref(a, 3, UP), slot_ref(a, 2, UP), right)
         if a != 3:
             declare(("FL", a), slot_ref(a, 1, DOWN), slot_ref(a, 2, DOWN), left)
-        if a % 2 == 0:
-            declare(("r", a), g_send.at[a * SIDE + 2, UP], x_rel_a.at[a // 2], right)
-            declare(("l", a), g_send.at[a * SIDE + 2, DOWN], x_rel_b.at[a // 2], left)
+        if a != 1:
+            declare(("r", a), g_send.at[a * SIDE + 2, UP], x_rel_a.at[a], right)
+        if a != 3:
+            declare(("l", a), g_send.at[a * SIDE + 2, DOWN], x_rel_b.at[a], left)
     for h in range(2):
         declare(("U", h), slot_ref(0, 0, halves[h]), slot_ref(3, 0, halves[h]), above)
         declare(("D", h), slot_ref(0, 0, halves[h]), slot_ref(1, 0, halves[h]), below)
@@ -121,12 +140,12 @@
         declare(("zd", h), z_send.at[3, halves[h]], z_in_r.at[halves[h]], below)
     declare(("VU",), slot_ref(0, 2, DOWN), slot_ref(3, 2, DOWN), above)
     declare(("VD",), slot_ref(0, 2, UP), slot_ref(1, 2, UP), below)
-    declare(("yu",), g_send.at[SIDE + 2], z_far.at[0], above)
-    declare(("yd",), g_send.at[3 * SIDE + 2], z_far.at[1], below)
+    declare(("yu",), g_send.at[SIDE + 2, UP], z_far.at[UP], above)
+    declare(("yd",), g_send.at[3 * SIDE + 2, DOWN], z_far.at[DOWN], below)
     declare(("FU",), slot_ref(3, 0, UP), slot_ref(2, 0, UP), above)
     declare(("FD",), slot_ref(1, 0, DOWN), slot_ref(2, 0, DOWN), below)
-    declare(("zr",), z_send.at[2, UP], z_rel_a, above)
-    declare(("zl",), z_send.at[2, DOWN], z_rel_b, below)
+    declare(("zr",), z_send.at[2, UP], z_rel.at[UP], above)
+    declare(("zl",), z_send.at[2, DOWN], z_rel.at[DOWN], below)
 
     def start(*names):
         for name in names:
@@ -268,8 +287,8 @@
     weigh[...] = jnp.zeros_like(weigh)
     dq_cols[...] = jnp.zeros_like(dq_cols)
 
-    def take_in(slot):
-        for n in range(TILES):
+    def take_in(slot, tiles=range(TILES)):
+        for n in tiles:
             tile = pl.ds(n * BLK, BLK)
             s = scores[slot, :, tile].reshape(CHUNK // 8, 8, BLK)
             d = dprobs[slot, :, tile].reshape(CHUNK // 8, 8, BLK)
@@ -363,7 +382,9 @@
             tile = pl.ds(n * WIDE, WIDE)
             scores[slot, :, tile] = dot(keys, q_cols[:, tile])
             dprobs[slot, :, tile] = dot(values, w_cols[:, tile])
-        take_in(slot)
+            if n:
+                take_in(slot, (2 * n - 2, 2 * n - 1))
+        take_in(slot, (TILES - 2, TILES - 1))
         return carry
 
     lax.fori_loop(0, MEMBERS, gather_step, 0)
@@ -378,8 +399,8 @@
         peak[:, tile] = jnp.broadcast_to(top + jnp.log2(mass) * (1.0 / c), (8, BLK))
         weigh[:, tile] = jnp.broadcast_to(delta, (8, BLK))
 
-    def probabilities(slot):
-        for n in range(TILES):
+    def probabilities(slot, tiles=range(TILES)):
+        for n in tiles:
             tile = pl.ds(n * BLK, BLK)
             s = scores[slot, :, tile].reshape(CHUNK // 8, 8, BLK)
             d = dprobs[slot, :, tile].reshape(CHUNK // 8, 8, BLK)
@@ -404,102 +425,76 @@
             own_grad[i, :, VALUES] = d_values[:BLK]
             give[i, :, KEYS] = d_keys[BLK:].astype(BF16)
             give[i, :, VALUES] = d_values[BLK:].astype(BF16)
-        spread(2, give, table_c)
-
-    def keep(a, b, h):
-        g_send[a * SIDE + b, halves[h]] = g_tmp[halves[h]].astype(BF16)
-
-    def join_right(a):
-        arrived(("r", a))
-        g_send[a * SIDE + 1, UP] = (g_hold[a] + x_rel_a[a // 2].astype(F32)).astype(BF16)
-        start(("gr", a, 0))
-
-    def join_left(a):
-        arrived(("l", a))
-        g_send[a * SIDE + 3, DOWN] = (g_hold[a + 1] + x_rel_b[a // 2].astype(F32)).astype(BF16)
-        start(("gl", a, 1))
+
+    def joins(a, b, h):
+        return (b == 1 and h == 0 and a != 1) or (b == 3 and h == 1 and a != 3)
+
+    def put_by(a, b):
+        if b == 0:
+            x_sum[a] = g_tmp[...]
+        elif (a, b) != (0, 2):
+            for h in range(2):
+                if joins(a, b, h):
+                    g_hold[2 * a + b // 2] = g_tmp[halves[h]]
+                else:
+                    g_send[a * SIDE + b, halves[h]] = g_tmp[halves[h]].astype(BF16)
 
     def x_combined(a, h):
         arrived(("gr", a, h), ("gl", a, h))
         half = halves[h]
         return x_sum[a, half] + x_in_l[a, half].astype(F32) + x_in_r[a, half].astype(F32)
 
-    def reduce_events(p):
-        a, b = REDUCE_ORDER[p]
-        if b == 0:
-            x_sum[a] = g_tmp[...]
-        elif (a, b) == (0, 2):
-            arrived(("yu",), ("yd",))
-            g_send[2] = (g_tmp[...] + z_far[0].astype(F32) + z_far[1].astype(F32)).astype(BF16)
-        elif a % 2 or b == 2:
-            keep(a, b, 0)
-            keep(a, b, 1)
-        elif b == 1:
-            keep(a, 1, 1)
-            g_hold[a] = g_tmp[UP]
+    def reduce_event(kind, a=0, h=0):
+        half = halves[h]
+        if kind == "far":
+            if a == 0:
+                arrived(("yu",), ("yd",))
+                g_send[2] = (g_tmp[...] + z_far[...].astype(F32)).astype(BF16)
+            start(("yu",) if a == 1 else ("r", a), ("yd",) if a == 3 else ("l", a))
+        elif kind in ("gr", "gl"):
+            b, relay, landed = (1, "r", x_rel_a) if kind == "gr" else (3, "l", x_rel_b)
+            if joins(a, b, h):
+                arrived((relay, a))
+                g_send[a * SIDE + b, half] = (g_hold[2 * a + b // 2] + landed[a].astype(F32)).astype(BF16)
+            start((kind, a, h))
+        elif kind == "z":
+            value = x_combined(a, h)
+            if (a, h) == (1, 0):
+                arrived(("zr",))
+                value = value + z_rel[half].astype(F32)
+            elif (a, h) == (3, 1):
+                arrived(("zl",))
+                value = value + z_rel[half].astype(F32)
+            z_send[a, half] = value.astype(BF16)
+            start({1: ("zu", h), 2: ("zr",) if h == 0 else ("zl",), 3: ("zd", h)}[a])
+        elif kind == "own":
+            own_grads()
+        elif kind == "spread":
+            spread(2, give, table_c)
         else:
-            keep(a, 3, 0)
-            g_hold[a + 1] = g_tmp[DOWN]
-        if p == 0:
-            start(("r", 2), ("l", 2))
-        elif p == 1:
-            start(("yd",))
-        elif p == 2:
-            start(("yu",))
-        elif p == 3:
-            start(("gr", 2, 1))
-        elif p == 4:
-            start(("gl", 2, 0))
-            join_right(2)
-            join_left(2)
-        elif p == 5:
-            own_grads()
-        elif p == 6:
-            start(("gr", 1, 1))
-        elif p == 7:
-            start(("gr", 3, 0), ("gr", 1, 0), ("gr", 3, 1))
-        elif p == 8:
-            start(("gl", 1, 1))
-        elif p == 9:
-            start(("gl", 3, 0), ("gl", 1, 0), ("gl", 3, 1))
-            for h in range(2):
-                z_send[2, halves[h]] = x_combined(2, h).astype(BF16)
-            start(("zr",), ("zl",))
-        elif p == 12:
-            start(("r", 0), ("l", 0))
-            z_send[1, DOWN] = x_combined(1, 1).astype(BF16)
-            start(("zu", 1))
-            z_send[3, UP] = x_combined(3, 0).astype(BF16)
-            start(("zd", 0))
-        elif p == 13:
-            start(("gr", 0, 1))
             every(lambda k: spread_copy(2, give, table_c, k).wait_recv())
             deliver(3, table_c, send_d, partner_grad)
-        elif p == 14:
-            start(("gl", 0, 0))
-            join_right(0)
-            join_left(0)
-            value = x_combined(1, 0)
-            arrived(("zr",))
-            z_send[1, UP] = (value + z_rel_a[...].astype(F32)).astype(BF16)
-            start(("zu", 0))
-            value = x_combined(3, 1)
-            arrived(("zl",))
-            z_send[3, DOWN] = (value + z_rel_b[...].astype(F32)).astype(BF16)
-            start(("zd", 1))
 
     def reduce_step(p, carry):
         slot = slot_at(REDUCE_ORDER, p)
-        probabilities(slot)
-        g_tmp[:, KEYS] = dot(ds_low[...], q_rows[...])
-        g_tmp[:, VALUES] = dot(p_low[...], w_rows[...])
+        keys = kv[slot, :, KEYS]
+        d_keys = jnp.zeros((CHUNK, HD), F32)
+        d_values = jnp.zeros((CHUNK, HD), F32)
         for n in range(ROWS // WIDE):
-            add_query_grad(kv[slot, :, KEYS], pl.ds(n * WIDE, WIDE))
+            tile = pl.ds(n * WIDE, WIDE)
+            probabilities(slot, (2 * n, 2 * n + 1))
+            d_keys = d_keys + dot(ds_low[:, tile], q_rows[tile, :])
+            d_values = d_values + dot(p_low[:, tile], w_rows[tile, :])
+            add_query_grad(keys, tile)
+        g_tmp[:, KEYS] = d_keys
+        g_tmp[:, VALUES] = d_values
 
         for k in range(MEMBERS):
             @pl.when(p == k)
             def _(k=k):
-                reduce_events(k)
+                put_by(*REDUCE_ORDER[k])
+                for event in REDUCE_EVENTS[k]:
+                    reduce_event(*event)
 
         return carry
 
@@ -534,6 +529,17 @@
     every(lambda k: deliver_copy(3, send_d, partner_grad, k).wait_send())
     for cp in counts:
         cp.wait_send()
+
+
+def write_out(query, stream, prompt, query_out, stream_out, prompt_out, sem):
+    copies = [
+        pltpu.make_async_copy(src, dst, sem.at[k])
+        for k, (src, dst) in enumerate(((query, query_out), (stream, stream_out), (prompt, prompt_out)))
+    ]
+    for cp in copies:
+        cp.start()
+    for cp in copies:
+        cp.wait()
 
 
 def local(query, resp_kv, prompt_kv, grad_out, rewards, lengths, block_order):
@@ -577,18 +583,17 @@
             pltpu.VMEM((HD, ROWS), F32),
             pltpu.VMEM(pair, F32),
             pltpu.VMEM((MEMBERS, *pair), BF16),
-            pltpu.VMEM((4, *half), F32),
-            pltpu.VMEM((2, *half), BF16),
-            pltpu.VMEM((2, *half), BF16),
+            pltpu.VMEM((2 * SIDE, *half), F32),
+            pltpu.VMEM((SIDE, *half), BF16),
+            pltpu.VMEM((SIDE, *half), BF16),
             pltpu.VMEM((SIDE, *pair), BF16),
             pltpu.VMEM((SIDE, *pair), BF16),
             pltpu.VMEM((SIDE, *pair), F32),
             pltpu.VMEM((SIDE, *pair), BF16),
-            pltpu.VMEM(half, BF16),
-            pltpu.VMEM(half, BF16),
             pltpu.VMEM(pair, BF16),
             pltpu.VMEM(pair, BF16),
-            pltpu.VMEM((2, *pair), BF16),
+            pltpu.VMEM(pair, BF16),
+            pltpu.VMEM(pair, BF16),
             pltpu.VMEM(pieces, BF16),
             pltpu.VMEM(pieces, BF16),
             pltpu.VMEM(blocks, BF16),
@@ -615,7 +620,20 @@
         query[0], resp_kv[0].reshape(blocks), prompt_kv[0], grad_out[0],
         rewards[0], lengths[0], block_order[0],
     )
-    return grads[0][None], grads[1].reshape(1, *pair), grads[2][None]
+    outs = pl.pallas_call(
+        write_out,
+        name="write_out",
+        out_shape=(
+            jax.ShapeDtypeStruct(wide, BF16),
+            jax.ShapeDtypeStruct(blocks, BF16),
+            jax.ShapeDtypeStruct(pair, BF16),
+        ),
+        in_specs=[vmem] * 3,
+        out_specs=(hbm,) * 3,
+        scratch_shapes=[pltpu.SemaphoreType.DMA((3,))],
+        compiler_params=pltpu.CompilerParams(vmem_limit_bytes=2**20),
+    )(*grads)
+    return outs[0][None], outs[1].reshape(1, *pair), outs[2][None]
 
 
 def solution(mesh):

time: 63.3 us -> 61.8 us (0.976); the launches traced: 63.2 us -> 60.8 us
  local copies, waits for them, and re-layouts: 2.04 us -> 0 us
    unnamed x3 -> x0, local copies, waits for them, and re-layouts: 2.04 us -> none
    pallas_call x1, Pallas kernels: 60.6 us -> 59.4 us  [local(): pl.pallas_call(kernel, name='attention_step', out_shape=(pltpu.VMEM(wide,...]
    pallas_call x0 -> x1, Pallas kernels: none -> 0.83 us  [local(): pl.pallas_call(write_out, name='write_out', out_shape=(jax.ShapeDtypeStru...]
where the time goes in v1:
time: 61.8 us; the launch traced here: 60.8 us
  Pallas kernels  60.2 us (97%)
  between operations  0.64 us (1%)
    pallas_call x1, Pallas kernels, local(): pl.pallas_call(kernel, name='attention_step', out_shape=(pltpu.VMEM(wide,...  59.4 us

profile of v1, /device:TPU:2, one launch (start us, length us, event | category | flops | bytes accessed | tf_op | source)
XLA Modules:
  0.0 60.8 jit_solution(17435118571248962481)
XLA Ops:
  0.6 59.4 %attention_step.1 = (bf16[256,640]{1,0:T(8,128)(2,1)S(1)}, bf16[2,128,256]{2,1,0:T(8,128)(2,1)S(1)}, bf16[256,256]{1,0:T(8,128)(2,1)S(1)}) custom-call(bf16[256,640]{1,0:T(8,128)(2,1)} %bitcast.10, bf16[2,128,256]{2,1,0:T(8,128)(2,1)} %bitcast.12, bf16[256,256]{1,0:T(8,128)(2,1)} %bitcast.13, bf16[256,640]{1,0:T(8,128)(2,1)} %bitcast.11, f32[16]{0:T(128)} %bitcast.14, ...), custom_call_target="tpu_custom_call" | custom-call | tf_op jit(solution)/shard_map/attention_step/pallas_call | solution.py:553
  60.0 0.8 %write_out.1 = (bf16[256,640]{1,0:T(8,128)(2,1)}, bf16[2,128,256]{2,1,0:T(8,128)(2,1)}, bf16[256,256]{1,0:T(8,128)(2,1)}) custom-call(bf16[256,640]{1,0:T(8,128)(2,1)S(1)} %get-tuple-element.9.query, bf16[2,128,256]{2,1,0:T(8,128)(2,1)S(1)} %get-tuple-element.10.stream, bf16[256,256]{1,0:T(8,128)(2,1)S(1)} %get-tuple-element.11.prompt), custom_call_target="tpu_custom_call" | custom-call | tf_op jit(solution)/shard_map/write_out/pallas_call | solution.py:623

commit v2 on v1

--- a/solution.py
+++ b/solution.py
@@ -40,18 +40,18 @@
 )
 REDUCE_EVENTS = (
     (("far", 2),),
-    (("far", 3),),
+    (("far", 3), ("own",), ("spread",)),
     (("far", 1),),
     (("gr", 2, 1),),
     (("gl", 2, 0), ("gr", 2, 0), ("gl", 2, 1)),
-    (("own",), ("spread",)),
+    (),
     (("gr", 1, 1),),
     (("gr", 3, 0), ("gr", 1, 0), ("gr", 3, 1)),
     (("gl", 1, 1),),
     (("gl", 3, 0), ("gl", 1, 0), ("gl", 3, 1), ("z", 2, 0), ("z", 2, 1)),
+    (("deliver",),),
     (),
-    (),
-    (("far", 0), ("z", 1, 1), ("z", 3, 0), ("deliver",)),
+    (("far", 0), ("z", 1, 1), ("z", 3, 0)),
     (("gr", 0, 1),),
     (("gl", 0, 0), ("z", 1, 0), ("z", 3, 1), ("gr", 0, 0), ("gl", 0, 1)),
     (),

time: 61.8 us -> 60.5 us (0.979)
  Pallas kernels: 60.2 us -> 59.3 us
    pallas_call x1, Pallas kernels: 59.4 us -> 58.5 us  [local(): pl.pallas_call(kernel, name='attention_step', out_shape=(pltpu.VMEM(wide,...]
where the time goes in v2:
time: 60.5 us; the launch traced here: 60 us
  Pallas kernels  59.3 us (98%)
  between operations  0.64 us (1%)
    pallas_call x1, Pallas kernels, local(): pl.pallas_call(kernel, name='attention_step', out_shape=(pltpu.VMEM(wide,...  58.5 us

profile of v2, /device:TPU:2, one launch (start us, length us, event | category | flops | bytes accessed | tf_op | source)
XLA Modules:
  0.0 60.0 jit_solution(3873838717539894938)
XLA Ops:
  0.6 58.5 %attention_step.1 = (bf16[256,640]{1,0:T(8,128)(2,1)S(1)}, bf16[2,128,256]{2,1,0:T(8,128)(2,1)S(1)}, bf16[256,256]{1,0:T(8,128)(2,1)S(1)}) custom-call(bf16[256,640]{1,0:T(8,128)(2,1)} %bitcast.10, bf16[2,128,256]{2,1,0:T(8,128)(2,1)} %bitcast.12, bf16[256,256]{1,0:T(8,128)(2,1)} %bitcast.13, bf16[256,640]{1,0:T(8,128)(2,1)} %bitcast.11, f32[16]{0:T(128)} %bitcast.14, ...), custom_call_target="tpu_custom_call" | custom-call | tf_op jit(solution)/shard_map/attention_step/pallas_call | solution.py:553
  59.1 0.8 %write_out.1 = (bf16[256,640]{1,0:T(8,128)(2,1)}, bf16[2,128,256]{2,1,0:T(8,128)(2,1)}, bf16[256,256]{1,0:T(8,128)(2,1)}) custom-call(bf16[256,640]{1,0:T(8,128)(2,1)S(1)} %get-tuple-element.9.query, bf16[2,128,256]{2,1,0:T(8,128)(2,1)S(1)} %get-tuple-element.10.stream, bf16[256,256]{1,0:T(8,128)(2,1)S(1)} %get-tuple-element.11.prompt), custom_call_target="tpu_custom_call" | custom-call | tf_op jit(solution)/shard_map/write_out/pallas_call | solution.py:623
